TPU v7x, 32 devices: a whole 2x2x4 slice. The times are simulated.
32 devices in a mesh: heads: 4 (over x, core), ctx: 8 (over z, y).
Axes of the slice: x: 2, y: 2, z: 4, core: 2. Of those that a mesh axis runs over, the one named last changes fastest.
Arguments:
- queries: bfloat16 [1536, 2048], P('ctx', 'heads'), may hold values from -6 to 6
- key_states: bfloat16 [1536, 512], P('ctx', 'heads'), may hold values from -6 to 6
- value_states: bfloat16 [1536, 512], P('ctx', 'heads'), may hold values from -6 to 6
- attention_out: bfloat16 [1536, 2048], P('ctx', 'heads'), may hold values from -2 to 2
- out_grad: bfloat16 [1536, 2048], P('ctx', 'heads'), may hold values from -6 to 6
- log_sum_exp: float32 [16, 1536], P('heads', 'ctx'), may hold values from 0 to 16, as said below
- block_counts: int32 [8], replicated, may hold values from 1 to 3, as said below
- w_query: bfloat16 [4096, 2048], P(None, 'heads'), may hold values from -0.09375 to 0.09375
- w_key: bfloat16 [4096, 512], P(None, 'heads'), may hold values from -0.09375 to 0.09375
- w_value: bfloat16 [4096, 512], P(None, 'heads'), may hold values from -0.09375 to 0.09375
Outputs:
- input_grad: bfloat16 [1536, 4096], P('ctx', 'heads')
- key_grad: float32 [1536, 512], P('ctx', 'heads')
- value_grad: float32 [1536, 512], P('ctx', 'heads')
Inputs may be any that keep to these rules, and one draw needn't show every extreme that they name: `block_counts`: one entry equals 3. `log_sum_exp`: finite offsets of each row's scores.
All inputs are finite; a program needn't handle non-finite values.
Results may differ from a plain program's by a relative error of at most 0.0063.
Values may be sent and summed in bfloat16 or wider, within the bound.
A program may use at most 128 MiB of HBM per device.

v0:
```python
import math
import jax
import jax.numpy as jnp
from jax import lax
from jax.sharding import PartitionSpec as P

BLOCK = 64


def key_span(row_count, capacity):
    shards = row_count // capacity
    per_step = max(1, min(shards, 512 // capacity))
    while shards % per_step:
        per_step = per_step - 1
    return per_step * capacity


def row_info(row_index, lengths, offsets, capacity):
    device = row_index // capacity
    onehot = device[:, None] == jnp.arange(lengths.shape[0], dtype=jnp.int32)[None, :]
    length = jnp.sum(jnp.where(onehot, lengths[None, :], 0), axis=1)
    offset = jnp.sum(jnp.where(onehot, offsets[None, :], 0), axis=1)
    within = row_index - device * capacity
    return (offset + within, within < length)


def tile_grads(
    query_blk,
    grad_blk,
    norm_blk,
    delta_blk,
    query_pos,
    query_live,
    key_blk,
    value_blk,
    key_pos,
    key_live,
    score_scale,
):
    scores = (
        jnp.einsum("qgd,kd->gqk", query_blk, key_blk, preferred_element_type=jnp.float32)
        * score_scale
    )
    visible = query_live[:, None] & key_live[None, :] & (key_pos[None, :] <= query_pos[:, None])
    probability = jnp.where(visible[None], jnp.exp(scores - norm_blk.T[:, :, None]), 0.0)
    prob_grad = jnp.einsum("qgd,kd->gqk", grad_blk, value_blk, preferred_element_type=jnp.float32)
    score_grad = probability * (prob_grad - delta_blk.T[:, :, None])
    return (probability.astype(jnp.bfloat16), score_grad.astype(jnp.bfloat16))


def on_device(
    queries,
    key_states,
    value_states,
    attention_out,
    out_grad,
    log_sum_exp,
    block_counts,
    w_query,
    w_key,
    w_value,
):
    capacity = key_states.shape[0]
    head_dim = key_states.shape[1]
    group = queries.shape[1] // head_dim
    score_scale = 1.0 / math.sqrt(head_dim)
    own_index = lax.axis_index("ctx")
    lengths = block_counts * BLOCK
    offsets = jnp.cumsum(lengths) - lengths
    own_rows = own_index * capacity + jnp.arange(capacity, dtype=jnp.int32)
    own_pos, own_live = row_info(own_rows, lengths, offsets, capacity)
    query_heads = queries.reshape(capacity, group, head_dim)
    grad_heads = out_grad.reshape(capacity, group, head_dim)
    output_heads = attention_out.reshape(capacity, group, head_dim)
    delta_rows = jnp.sum(grad_heads.astype(jnp.float32) * output_heads.astype(jnp.float32), axis=2)
    norm_rows = log_sum_exp.T
    zero_rows = jnp.zeros((capacity, group, head_dim), jnp.float32)
    zero_own = jnp.zeros((capacity, head_dim), jnp.float32)
    key_piece = lax.all_gather(key_states, "ctx", axis=0, tiled=True)
    value_piece = lax.all_gather(value_states, "ctx", axis=0, tiled=True)
    span = key_span(key_piece.shape[0], capacity)

    def step(block_num, query_grad):
        begin_row = block_num * span
        key_blk = lax.dynamic_slice_in_dim(key_piece, begin_row, span, 0)
        value_blk = lax.dynamic_slice_in_dim(value_piece, begin_row, span, 0)
        key_pos, key_live = row_info(
            begin_row + jnp.arange(span, dtype=jnp.int32), lengths, offsets, capacity
        )

        def compute():
            prob_b, grad_b = tile_grads(
                query_heads,
                grad_heads,
                norm_rows,
                delta_rows,
                own_pos,
                own_live,
                key_blk,
                value_blk,
                key_pos,
                key_live,
                score_scale,
            )
            return score_scale * jnp.einsum(
                "gqk,kd->qgd", grad_b, key_blk, preferred_element_type=jnp.float32
            )

        terms = compute()
        return query_grad + terms

    query_grad = lax.fori_loop(0, key_piece.shape[0] // span, step, zero_rows)
    norm_all, delta_all = (
        lax.all_gather(norm_rows, "ctx", axis=0, tiled=True),
        lax.all_gather(delta_rows, "ctx", axis=0, tiled=True),
    )
    query_piece = lax.all_gather(queries, "ctx", axis=0, tiled=True)
    grad_piece = lax.all_gather(out_grad, "ctx", axis=0, tiled=True)
    fold_span = key_span(query_piece.shape[0], capacity)

    def step(block_num, state):
        key_acc, value_acc = state
        begin_row = block_num * fold_span
        query_blk = lax.dynamic_slice_in_dim(query_piece, begin_row, fold_span, 0).reshape(
            fold_span, group, head_dim
        )
        grad_blk = lax.dynamic_slice_in_dim(grad_piece, begin_row, fold_span, 0).reshape(
            fold_span, group, head_dim
        )
        norm_blk = lax.dynamic_slice_in_dim(norm_all, begin_row, fold_span, 0)
        delta_blk = lax.dynamic_slice_in_dim(delta_all, begin_row, fold_span, 0)
        query_pos, query_live = row_info(
            begin_row + jnp.arange(fold_span, dtype=jnp.int32), lengths, offsets, capacity
        )

        def compute():
            prob_b, grad_b = tile_grads(
                query_blk,
                grad_blk,
                norm_blk,
                delta_blk,
                query_pos,
                query_live,
                key_states,
                value_states,
                own_pos,
                own_live,
                score_scale,
            )
            return (
                score_scale
                * jnp.einsum("gqk,qgd->kd", grad_b, query_blk, preferred_element_type=jnp.float32),
                jnp.einsum("gqk,qgd->kd", prob_b, grad_blk, preferred_element_type=jnp.float32),
            )

        terms = compute()
        return (key_acc + terms[0], value_acc + terms[1])

    key_grad, value_grad = lax.fori_loop(
        0, query_piece.shape[0] // fold_span, step, (zero_own, zero_own)
    )
    query_flat = query_grad.reshape(capacity, group * head_dim).astype(jnp.bfloat16)
    partial_input = jnp.einsum("rc,mc->rm", query_flat, w_query, preferred_element_type=jnp.float32)
    partial_input = partial_input + jnp.einsum(
        "rc,mc->rm", key_grad.astype(jnp.bfloat16), w_key, preferred_element_type=jnp.float32
    )
    partial_input = partial_input + jnp.einsum(
        "rc,mc->rm", value_grad.astype(jnp.bfloat16), w_value, preferred_element_type=jnp.float32
    )
    input_part = lax.psum_scatter(partial_input, "heads", scatter_dimension=1, tiled=True)
    return (input_part.astype(jnp.bfloat16), key_grad, value_grad)


def solution(mesh):
    return jax.shard_map(
        on_device,
        mesh=mesh,
        in_specs=(
            P("ctx", "heads"),
            P("ctx", "heads"),
            P("ctx", "heads"),
            P("ctx", "heads"),
            P("ctx", "heads"),
            P("heads", "ctx"),
            P(),
            P(None, "heads"),
            P(None, "heads"),
            P(None, "heads"),
        ),
        out_specs=(P("ctx", "heads"), P("ctx", "heads"), P("ctx", "heads")),
        check_vma=False,
    )
```

profile of v0, /device:TPU:0, one launch (start us, length us, event | category | flops | bytes accessed | tf_op | source)
XLA Modules:
  0.0 253.6 jit_solution(5064324992087366843)
XLA Ops:
  8.7 1.0 reshape.280
  9.7 1.0 copy_bitcast_fusion
  12.7 0.7 select_reduce_fusion.4
  15.1 34.2 %all_gather.18 = bf16[1536,128]{1,0:T(8,128)(2,1)S(1)} all-gather(bf16[192,128]{1,0:T(8,128)(2,1)} %param.15), channel_id=1, replica_groups=mesh['heads'=4,'ctx'=8] {'ctx'}, dimensions={0}, use_global_device_ids=true | all-gather | bytes 442368 | tf_op jit(solution)/shard_map/all_gather | solution.py:79
  49.3 33.4 %all_gather.19 = bf16[1536,128]{1,0:T(8,128)(2,1)} all-gather(bf16[192,128]{1,0:T(8,128)(2,1)S(1)} %copy-done.3), channel_id=1, replica_groups=mesh['heads'=4,'ctx'=8] {'ctx'}, dimensions={0}, use_global_device_ids=true | all-gather | bytes 442368 | tf_op jit(solution)/shard_map/all_gather | solution.py:80
  82.7 18.1 %while.34 = (s32[]{:T(128)}, f32[192,4,128]{2,0,1:T(8,128)S(1)}, bf16[1536,128]{1,0:T(8,128)(2,1)S(1)}, pred[192]{0:T(512)(128)(4,1)}, s32[8]{0:T(128)}, /*index...) while((s32[]{:T(128)}, f32[192,4,128]{2,0,1:T(8,128)S(1)}, ...), condition=%wide.region_7.8_spmd.clone, body=%wide.region_4.7_spmd.clone.sunk | while | flops 228805248 | bytes 4005340 | solution.py:112
  83.5 0.8 compare_and_fusion.4
  84.3 1.4 fusion.93
  85.7 1.5 fusion.94
  87.3 0.7 select_reduce_fusion.8
  88.0 0.8 compare_and_fusion.4
  88.8 1.4 fusion.93
  90.2 1.5 fusion.94
  92.5 0.8 compare_and_fusion.4
  93.4 1.4 fusion.93
  94.7 1.5 fusion.94
  97.1 0.8 compare_and_fusion.4
  97.9 1.4 fusion.93
  99.3 1.5 fusion.94
  100.9 30.6 %all-gather.1 = f32[8,192,4]{1,2,0:T(4,128)S(1)} all-gather(f32[1,192,4]{1,2,0:T(4,128)S(1)} %copy.55), channel_id=1, replica_groups=mesh['heads'=4,'ctx'=8] {'ctx'}, dimensions={0}, use_global_device_ids=true | all-gather | bytes 27648 | tf_op jit(solution)/shard_map/all_gather | solution.py:115
  132.3 30.6 %all-gather = f32[8,192,4]{1,2,0:T(4,128)S(1)} all-gather(f32[1,192,4]{1,2,0:T(4,128)S(1)} %bitcast.173), channel_id=1, replica_groups=mesh['heads'=4,'ctx'=8] {'ctx'}, dimensions={0}, use_global_device_ids=true | all-gather | bytes 27648 | tf_op jit(solution)/shard_map/all_gather | solution.py:114
  163.6 5.4 %fusion.46 = f32[192,4096]{1,0:T(8,128)} fusion(bf16[4096,512]{1,0:T(8,128)(2,1)} %param.21, f32[192,4,128]{2,0,1:T(8,128)S(1)} %get-tuple-element.600), kind=kOutput, calls=%fused_computation.72 | convolution fusion | flops 805404672 | bytes 7733248 | tf_op jit(solution)/shard_map/rc,mc->rm/dot_general | solution.py:163
  168.9 31.9 %while.35 = (s32[]{:T(128)}, f32[192,128]{1,0:T(8,128)S(1)}, f32[192,128]{1,0:T(8,128)}, s32[8]{0:T(128)}, pred[192]{0:T(512)(128)(4,1)}, /*index=5*/s32[192]{0:...) while((s32[]{:T(128)}, f32[192,128]{1,0:T(8,128)S(1)}, ...), condition=%wide.region_11.12_spmd.clone, body=%wide.region_8.11_spmd.clone.sunk | while | flops 304425600 | bytes 8972294 | solution.py:159
  168.9 0.7 select_reduce_fusion.9
  169.7 0.8 compare_and_fusion.5
  170.5 1.2 constant_dynamic-slice_fusion.3
  171.9 1.3 dynamic-slice_bitcast_fusion.3
  173.2 1.2 fusion.104
  174.6 1.0 fusion.106
  177.0 0.8 compare_and_fusion.5
  177.8 1.2 constant_dynamic-slice_fusion.3
  179.2 1.3 dynamic-slice_bitcast_fusion.3
  180.5 1.2 fusion.104
  182.0 1.9 fusion.106
  185.2 0.8 compare_and_fusion.5
  186.0 1.2 constant_dynamic-slice_fusion.3
  187.4 1.3 dynamic-slice_bitcast_fusion.3
  188.7 1.2 fusion.104
  190.2 1.9 fusion.106
  193.4 0.8 compare_and_fusion.5
  194.3 1.2 constant_dynamic-slice_fusion.3
  195.6 1.3 dynamic-slice_bitcast_fusion.3
  196.9 1.2 fusion.104
  198.4 1.9 fusion.106
  200.9 2.6 %convolution_add_fusion.1 = f32[192,4096]{1,0:T(8,128)S(1)} fusion(f32[192,4096]{1,0:T(8,128)} %fusion.46, bf16[4096,128]{1,0:T(8,128)(2,1)S(1)} %copy-done, f32[192,128]{1,0:T(8,128)S(1)} %get-tuple-element.598), kind=kOutput, calls=%fused_computation.70 | convolution fusion | flops 202137600 | bytes 7438336 | tf_op jit(solution)/shard_map/rc,mc->rm/dot_general | solution.py:164
  203.5 2.2 convolution_add_fusion
  205.8 39.4 %reduce-scatter.2.cloned.1.call-done = f32[192,1024]{1,0:T(8,128)} async-done(((f32[192,4096]{1,0:T(8,128)}), f32[192,1024]{1,0:T(8,128)}) %reduce-scatter.2.cloned.1.call-update) | async-done | bytes 786448 | tf_op jit(solution)/shard_map/reduce_scatter | solution.py:170
  245.1 1.9 convert_element_type.61
  (94 shorter events, 15.4 us)
Async XLA Ops:
  7.2 193.7 %copy-start = (bf16[4096,128]{1,0:T(8,128)(2,1)S(1)}, bf16[4096,128]{1,0:T(8,128)(2,1)}, u32[]{:S(2)}) copy-start(bf16[4096,128]{1,0:T(8,128)(2,1)} %param.22) | copy-start | bytes 3145732
  7.2 3.5 %copy-start.5 = (bf16[192,512]{1,0:T(8,128)(2,1)S(1)}, bf16[192,512]{1,0:T(8,128)(2,1)}, u32[]{:S(2)}) copy-start(bf16[192,512]{1,0:T(8,128)(2,1)} %param.14) | copy-start | bytes 589828
  7.2 4.2 %copy-start.9 = (s32[8]{0:T(128)S(1)}, s32[8]{0:T(128)}, u32[]{:S(2)}) copy-start(s32[8]{0:T(128)} %param.20) | copy-start | bytes 100
  7.2 7.4 %copy-start.7 = (bf16[192,512]{1,0:T(8,128)(2,1)S(1)}, bf16[192,512]{1,0:T(8,128)(2,1)}, u32[]{:S(2)}) copy-start(bf16[192,512]{1,0:T(8,128)(2,1)} %param.17) | copy-start | bytes 589828
  7.2 161.7 %all-gather.5.cloned.1.call-start = ((), (), s32[]{:S(2)}) async-start(), calls=%async_computation.1 | async-start | bytes 1769472 | tf_op jit(solution)/shard_map/all_gather | solution.py:117
  7.9 161.0 %all-gather.7.cloned.1.call-start = ((), (), s32[]{:S(2)}) async-start(), calls=%async_computation.2 | async-start | bytes 1769472 | tf_op jit(solution)/shard_map/all_gather | solution.py:118
  8.7 236.4 %reduce-scatter.2.cloned.1.call-start = ((), (), s32[]{:S(2)}) async-start(), calls=%async_computation.3 | async-start | bytes 3932160 | tf_op jit(solution)/shard_map/reduce_scatter | solution.py:170
  10.7 38.6 %copy-start.3 = (bf16[192,128]{1,0:T(8,128)(2,1)S(1)}, bf16[192,128]{1,0:T(8,128)(2,1)}, u32[]{:S(2)}) copy-start(bf16[192,128]{1,0:T(8,128)(2,1)} %param.16) | copy-start | bytes 147460
  11.4 71.3 %copy-start.8 = (f32[4,192]{1,0:T(4,128)S(1)}, f32[4,192]{1,0:T(4,128)}, u32[]{:S(2)}) copy-start(f32[4,192]{1,0:T(4,128)} %param.19) | copy-start | bytes 9220
  174.6 1.0 copy-start.6
  181.9 1.9 copy-start.6
  190.2 1.9 copy-start.6
  198.4 1.9 copy-start.6
  200.9 2.6 %copy-start.1 = (f32[192,128]{1,0:T(8,128)}, f32[192,128]{1,0:T(8,128)S(1)}, u32[]{:S(2)}) copy-start(f32[192,128]{1,0:T(8,128)S(1)} %get-tuple-element.598) | copy-start | bytes 294916
  200.9 2.6 %copy-start.2 = (f32[192,128]{1,0:T(8,128)S(1)}, f32[192,128]{1,0:T(8,128)}, u32[]{:S(2)}) copy-start(f32[192,128]{1,0:T(8,128)} %get-tuple-element.599) | copy-start | bytes 294916
  200.9 2.6 %copy-start.4 = (bf16[4096,128]{1,0:T(8,128)(2,1)S(1)}, bf16[4096,128]{1,0:T(8,128)(2,1)}, u32[]{:S(2)}) copy-start(bf16[4096,128]{1,0:T(8,128)(2,1)} %param.23) | copy-start | bytes 3145732
Sparse Core Ops, SparseCore 0:
  10.2 50.6 all-gather.4
  63.1 43.6 all-gather.6
  205.9 39.1 reduce-scatter.1
where the time goes:
time: 255 us; the launch traced here: 254 us
  blocking collectives  129 us (51%)
  waiting for transfers between devices  40.8 us (16%)
  matrix products  35.5 us (14%)
  other arithmetic  18 us (7%)
  local copies, waits for them, and re-layouts  16 us (6%)
  between operations  13.9 us (5%)
    reduce_scatter x1, waiting for transfers between devices, on_device(): lax.psum_scatter(partial_input, 'heads', scatter_dimension=1, tiled=True)  39.4 us
    all_gather x1, blocking collectives, on_device(): key_piece = lax.all_gather(key_states, 'ctx', axis=0, tiled=True)  34.2 us
    all_gather x1, blocking collectives, on_device(): value_piece = lax.all_gather(value_states, 'ctx', axis=0, tiled=True)  33.4 us
    all_gather x1, blocking collectives, on_device(): lax.all_gather(delta_rows, 'ctx', axis=0, tiled=True)  30.6 us
    all_gather x1, blocking collectives, on_device(): lax.all_gather(norm_rows, 'ctx', axis=0, tiled=True)  30.6 us
    dot_general x8, matrix products, tile_grads(): jnp.einsum('qgd,kd->gqk', query_blk, key_blk, preferred_element_type=jnp....  10.2 us
    dot_general x4, matrix products, compute(): jnp.einsum('gqk,qgd->kd', prob_b, grad_blk, preferred_element_type=jnp.fl...  6.56 us
    and x8, other arithmetic, tile_grads(): query_live[:, None] & key_live[None, :]  6.44 us
  transfers between devices with their start and end apart: 3, of which 1 were waited for; matrix products, arithmetic and copies ran while one was open for 12% of the time, Pallas kernels for 0%

commit v1 on v0

--- a/solution.py
+++ b/solution.py
@@ -3,8 +3,18 @@
 import jax.numpy as jnp
 from jax import lax
 from jax.sharding import PartitionSpec as P
+from jax.lax import all_gather
 
 BLOCK = 64
+
+
+def assign_block(a0, here_x):
+    raw_out = jnp.split(
+        all_gather(jnp.concatenate([a0, here_x], axis=1), "ctx", axis=0, tiled=True),
+        [a0.shape[1]],
+        axis=1,
+    )
+    return raw_out
 
 
 def key_span(row_count, capacity):
@@ -76,8 +86,7 @@
     norm_rows = log_sum_exp.T
     zero_rows = jnp.zeros((capacity, group, head_dim), jnp.float32)
     zero_own = jnp.zeros((capacity, head_dim), jnp.float32)
-    key_piece = lax.all_gather(key_states, "ctx", axis=0, tiled=True)
-    value_piece = lax.all_gather(value_states, "ctx", axis=0, tiled=True)
+    key_piece, value_piece = assign_block(key_states, value_states)
     span = key_span(key_piece.shape[0], capacity)
 
     def step(block_num, query_grad):

time: 255 us -> 225 us (0.88)
  blocking collectives: 129 us -> 97.1 us
  matrix products: 35.5 us -> 31 us
  local copies, waits for them, and re-layouts: 16 us -> 19.8 us
  other arithmetic: 18 us -> 21.7 us
    all_gather x2 -> x1, blocking collectives: 67.6 us -> 35.5 us  [assign_block(): all_gather(jnp.concatenate([a0, here_x], axis=1), 'ctx', axis=0, tiled=True)]
    dot_general x4, matrix products: 6.56 us -> 1.34 us  [compute(): jnp.einsum('gqk,qgd->kd', prob_b, grad_blk, preferred_element_type=jnp.fl...]
    while x8 -> x40, local copies, waits for them, and re-layouts: 0.02 us -> 3.73 us
  transfers between devices with their start and end apart: 3 -> 3, of which waited for: 1 -> 1; matrix products, arithmetic and copies ran while one was open for 12% -> 14% of each run, Pallas kernels for 0% -> 0%
where the time goes in v1:
time: 225 us; the launch traced here: 224 us
  blocking collectives  97.1 us (43%)
  waiting for transfers between devices  39.9 us (18%)
  matrix products  31 us (14%)
  other arithmetic  21.7 us (10%)
  local copies, waits for them, and re-layouts  19.8 us (9%)
  between operations  13.9 us (6%)
    reduce_scatter x1, waiting for transfers between devices, on_device(): lax.psum_scatter(partial_input, 'heads', scatter_dimension=1, tiled=True)  38.5 us
    all_gather x1, blocking collectives, assign_block(): all_gather(jnp.concatenate([a0, here_x], axis=1), 'ctx', axis=0, tiled=True)  35.5 us
    all_gather x1, blocking collectives, on_device(): lax.all_gather(norm_rows, 'ctx', axis=0, tiled=True)  31 us
    all_gather x1, blocking collectives, on_device(): lax.all_gather(delta_rows, 'ctx', axis=0, tiled=True)  30.6 us
    dot_general x8, matrix products, tile_grads(): jnp.einsum('qgd,kd->gqk', query_blk, key_blk, preferred_element_type=jnp....  11 us
    and x8, other arithmetic, tile_grads(): query_live[:, None] & key_live[None, :]  8.93 us
    dot_general x4, matrix products, compute(): jnp.einsum('gqk,kd->qgd', grad_b, key_blk, preferred_element_type=jnp.flo...  6.15 us
    reduce_sum x8, other arithmetic, row_info(): length = jnp.sum(jnp.where(onehot, lengths[None, :], 0), axis=1)  6.11 us
  transfers between devices with their start and end apart: 3, of which 1 were waited for; matrix products, arithmetic and copies ran while one was open for 14% of the time, Pallas kernels for 0%

profile of v1, /device:TPU:0, one launch (start us, length us, event | category | flops | bytes accessed | tf_op | source)
XLA Modules:
  0.0 224.1 jit_solution(4249954665444000589)
XLA Ops:
  8.7 1.6 copy_bitcast_fusion.1
  10.4 1.0 copy_bitcast_fusion
  15.2 0.8 pad_maximum_fusion
  16.0 35.5 %all_gather.15 = bf16[1536,256]{1,0:T(8,128)(2,1)S(1)} all-gather(bf16[192,256]{1,0:T(8,128)(2,1)S(1)} %pad_maximum_fusion), channel_id=1, replica_groups=mesh['heads'=4,'ctx'=8] {'ctx'}, dimensions={0}, use_global_device_ids=true | all-gather | bytes 884736 | tf_op jit(solution)/shard_map/all_gather | solution.py:13
  51.5 0.8 fusion.54
  52.3 18.5 %while.34 = (s32[]{:T(128)}, f32[192,4,128]{2,0,1:T(8,128)S(1)}, bf16[1536,128]{1,0:T(8,128)(2,1)}, pred[192]{0:T(512)(128)(4,1)}, s32[8]{0:T(128)}, /*index=5*/...) while((s32[]{:T(128)}, f32[192,4,128]{2,0,1:T(8,128)S(1)}, ...), condition=%wide.region_7.8_spmd.clone, body=%wide.region_4.7_spmd.clone.sunk | while | flops 228805248 | bytes 4004324 | solution.py:121
  52.3 0.8 select_reduce_fusion.8
  53.1 0.8 compare_and_fusion.4
  53.9 1.4 fusion.94
  55.4 1.5 fusion.95
  57.0 0.8 select_reduce_fusion.8
  57.8 0.8 compare_and_fusion.4
  58.6 1.4 fusion.94
  60.0 1.5 fusion.95
  61.6 0.8 select_reduce_fusion.8
  62.4 0.8 compare_and_fusion.4
  63.2 1.4 fusion.94
  64.6 1.5 fusion.95
  66.2 0.8 select_reduce_fusion.8
  67.0 0.8 compare_and_fusion.4
  67.8 1.4 fusion.94
  69.2 1.5 fusion.95
  70.8 31.0 %all-gather = f32[8,192,4]{1,2,0:T(4,128)S(1)} all-gather(f32[1,192,4]{1,2,0:T(4,128)S(1)} %bitcast.173), channel_id=1, replica_groups=mesh['heads'=4,'ctx'=8] {'ctx'}, dimensions={0}, use_global_device_ids=true | all-gather | bytes 27648 | tf_op jit(solution)/shard_map/all_gather | solution.py:123
  102.6 30.6 %all-gather.1 = f32[8,192,4]{1,2,0:T(4,128)S(1)} all-gather(f32[1,192,4]{1,2,0:T(4,128)S(1)} %copy.55), channel_id=1, replica_groups=mesh['heads'=4,'ctx'=8] {'ctx'}, dimensions={0}, use_global_device_ids=true | all-gather | bytes 27648 | tf_op jit(solution)/shard_map/all_gather | solution.py:124
  133.3 5.4 %fusion.46 = f32[192,4096]{1,0:T(8,128)} fusion(bf16[4096,512]{1,0:T(8,128)(2,1)} %param.21, f32[192,4,128]{2,0,1:T(8,128)S(1)} %get-tuple-element.600), kind=kOutput, calls=%fused_computation.72 | convolution fusion | flops 805404672 | bytes 7733248 | tf_op jit(solution)/shard_map/rc,mc->rm/dot_general | solution.py:172
  138.6 33.6 %while.35 = (s32[]{:T(128)}, f32[192,128]{1,0:T(8,128)S(1)}, f32[192,128]{1,0:T(8,128)}, s32[8]{0:T(128)}, pred[192]{0:T(512)(128)(4,1)}, /*index=5*/s32[192]{0:...) while((s32[]{:T(128)}, f32[192,128]{1,0:T(8,128)S(1)}, ...), condition=%wide.region_11.12_spmd.clone, body=%wide.region_8.11_spmd.clone.sunk | while | flops 304425600 | bytes 9955454 | solution.py:168
  138.7 0.8 select_reduce_fusion.9
  139.5 1.3 dynamic-slice_bitcast_fusion.3
  140.8 1.4 compare_and_fusion.5
  142.2 1.2 constant_dynamic-slice_fusion.3
  143.8 1.3 fusion.105
  147.1 0.8 select_reduce_fusion.9
  147.9 1.3 dynamic-slice_bitcast_fusion.3
  149.2 1.4 compare_and_fusion.5
  150.6 1.2 constant_dynamic-slice_fusion.3
  152.2 1.3 fusion.105
  156.3 1.3 dynamic-slice_bitcast_fusion.3
  157.6 1.4 compare_and_fusion.5
  159.0 1.2 constant_dynamic-slice_fusion.3
  160.6 1.3 fusion.105
  164.7 1.3 dynamic-slice_bitcast_fusion.3
  166.0 1.4 compare_and_fusion.5
  167.4 1.2 constant_dynamic-slice_fusion.3
  169.0 1.3 fusion.105
  172.3 2.6 %convolution_add_fusion.1 = f32[192,4096]{1,0:T(8,128)S(1)} fusion(f32[192,4096]{1,0:T(8,128)} %fusion.46, bf16[4096,128]{1,0:T(8,128)(2,1)S(1)} %copy-done, f32[192,128]{1,0:T(8,128)S(1)} %get-tuple-element.598), kind=kOutput, calls=%fused_computation.70 | convolution fusion | flops 202137600 | bytes 7438336 | tf_op jit(solution)/shard_map/rc,mc->rm/dot_general | solution.py:173
  174.9 2.2 convolution_add_fusion
  177.1 38.5 %reduce-scatter.2.cloned.1.call-done = f32[192,1024]{1,0:T(8,128)} async-done(((f32[192,4096]{1,0:T(8,128)}), f32[192,1024]{1,0:T(8,128)}) %reduce-scatter.2.cloned.1.call-update) | async-done | bytes 786448 | tf_op jit(solution)/shard_map/reduce_scatter | solution.py:179
  215.6 1.9 convert_element_type.61
  (127 shorter events, 17.2 us)
Async XLA Ops:
  7.2 165.1 %copy-start = (bf16[4096,128]{1,0:T(8,128)(2,1)S(1)}, bf16[4096,128]{1,0:T(8,128)(2,1)}, u32[]{:S(2)}) copy-start(bf16[4096,128]{1,0:T(8,128)(2,1)} %param.22) | copy-start | bytes 3145732
  7.2 4.2 %copy-start.5 = (bf16[192,512]{1,0:T(8,128)(2,1)S(1)}, bf16[192,512]{1,0:T(8,128)(2,1)}, u32[]{:S(2)}) copy-start(bf16[192,512]{1,0:T(8,128)(2,1)} %param.18) | copy-start | bytes 589828
  7.2 4.3 %copy-start.13 = (s32[8]{0:T(128)S(1)}, s32[8]{0:T(128)}, u32[]{:S(2)}) copy-start(s32[8]{0:T(128)} %param.20) | copy-start | bytes 100
  7.2 7.5 %copy-start.9 = (bf16[192,512]{1,0:T(8,128)(2,1)S(1)}, bf16[192,512]{1,0:T(8,128)(2,1)}, u32[]{:S(2)}) copy-start(bf16[192,512]{1,0:T(8,128)(2,1)} %param.17) | copy-start | bytes 589828
  7.2 131.4 %all-gather.5.cloned.1.call-start = ((), (), s32[]{:S(2)}) async-start(), calls=%async_computation.1 | async-start | bytes 1769472 | tf_op jit(solution)/shard_map/all_gather | solution.py:126
  7.9 130.7 %all-gather.7.cloned.1.call-start = ((), (), s32[]{:S(2)}) async-start(), calls=%async_computation.2 | async-start | bytes 1769472 | tf_op jit(solution)/shard_map/all_gather | solution.py:127
  8.7 206.9 %reduce-scatter.2.cloned.1.call-start = ((), (), s32[]{:S(2)}) async-start(), calls=%async_computation.3 | async-start | bytes 3932160 | tf_op jit(solution)/shard_map/reduce_scatter | solution.py:179
  10.4 4.8 %copy-start.6 = (bf16[192,128]{1,0:T(8,128)(2,1)S(1)}, bf16[192,128]{1,0:T(8,128)(2,1)}, u32[]{:S(2)}) copy-start(bf16[192,128]{1,0:T(8,128)(2,1)} %param.16) | copy-start | bytes 147460
  16.0 36.3 %copy-start.12 = (f32[4,192]{1,0:T(4,128)S(1)}, f32[4,192]{1,0:T(4,128)}, u32[]{:S(2)}) copy-start(f32[4,192]{1,0:T(4,128)} %param.19) | copy-start | bytes 9220
  138.6 4.7 %copy-start.10 = (f32[1536,4]{0,1:T(4,128)}, f32[1536,4]{0,1:T(4,128)S(1)}, u32[]{:S(2)}) copy-start(f32[1536,4]{0,1:T(4,128)S(1)} %get-tuple-element.1085) | copy-start | bytes 73732 | tf_op jit(solution)/shard_map/while
  143.8 1.3 copy-start.8
  145.2 0.9 copy-start.2
  146.1 1.0 copy-start.11
  146.4 0.6 copy-start.3
  147.0 4.7 %copy-start.10 = (f32[1536,4]{0,1:T(4,128)}, f32[1536,4]{0,1:T(4,128)S(1)}, u32[]{:S(2)}) copy-start(f32[1536,4]{0,1:T(4,128)S(1)} %get-tuple-element.1085) | copy-start | bytes 73732 | tf_op jit(solution)/shard_map/while
  152.2 1.3 copy-start.8
  153.6 0.9 copy-start.2
  154.5 1.0 copy-start.11
  154.8 0.6 copy-start.3
  155.5 4.7 %copy-start.10 = (f32[1536,4]{0,1:T(4,128)}, f32[1536,4]{0,1:T(4,128)S(1)}, u32[]{:S(2)}) copy-start(f32[1536,4]{0,1:T(4,128)S(1)} %get-tuple-element.1085) | copy-start | bytes 73732 | tf_op jit(solution)/shard_map/while
  160.6 1.3 copy-start.8
  162.0 0.9 copy-start.2
  162.9 1.0 copy-start.11
  163.2 0.6 copy-start.3
  163.9 4.7 %copy-start.10 = (f32[1536,4]{0,1:T(4,128)}, f32[1536,4]{0,1:T(4,128)S(1)}, u32[]{:S(2)}) copy-start(f32[1536,4]{0,1:T(4,128)S(1)} %get-tuple-element.1085) | copy-start | bytes 73732 | tf_op jit(solution)/shard_map/while
  169.0 1.3 copy-start.8
  170.4 0.9 copy-start.2
  171.3 1.0 copy-start.11
  171.6 0.6 copy-start.3
  172.3 2.6 %copy-start.1 = (f32[192,128]{1,0:T(8,128)}, f32[192,128]{1,0:T(8,128)S(1)}, u32[]{:S(2)}) copy-start(f32[192,128]{1,0:T(8,128)S(1)} %get-tuple-element.598) | copy-start | bytes 294916
  172.3 2.6 %copy-start.4 = (f32[192,128]{1,0:T(8,128)S(1)}, f32[192,128]{1,0:T(8,128)}, u32[]{:S(2)}) copy-start(f32[192,128]{1,0:T(8,128)} %get-tuple-element.599) | copy-start | bytes 294916
  172.3 2.6 %copy-start.7 = (bf16[4096,128]{1,0:T(8,128)(2,1)S(1)}, bf16[4096,128]{1,0:T(8,128)(2,1)}, u32[]{:S(2)}) copy-start(bf16[4096,128]{1,0:T(8,128)(2,1)} %param.23) | copy-start | bytes 3145732
Sparse Core Ops, SparseCore 0:
  10.2 50.9 all-gather.4
  63.4 43.5 all-gather.6
  177.3 38.3 reduce-scatter.1
